TPU v7x, 32 devices: a whole 2x2x4 slice. The times are simulated.
32 devices in a mesh: rows: 8 (over y, x, core), sub: 4 (over z).
Axes of the slice: x: 2, y: 2, z: 4, core: 2. Of those that a mesh axis runs over, the one named last changes fastest.
Arguments:
- u_fem: float32 [120, 524288], P(None, ('rows', 'sub')), may hold values from -600 to 600
- resid_fem: float32 [1, 524288], P(None, ('rows', 'sub')), may hold values from -60 to 60
- slot_map: int32 [32, 32], P(('rows', 'sub')), may hold values from 0 to 31, as said below
- restart: float32 [120, 40], replicated, may hold values from -0.5 to 0.5
- coeff: float32 [3, 120, 120], P(None, None, 'sub'), may hold values from -6 to 6
Outputs:
- new_basis: float32 [40, 524288], P(None, ('rows', 'sub'))
- next_vector: float32 [1, 524288], P(None, ('rows', 'sub'))
- new_coeff: float32 [3, 40, 120], replicated
Inputs may be any that keep to these rules, and one draw needn't show every extreme that they name: Each row of slot_map is a permutation of 0 to 31.
All inputs are finite; a program needn't handle non-finite values.
Results may differ from a plain program's by a relative error of at most 0.00015.
Values sent between devices are 32-bit elements; how exact they have to be, the bound alone decides.
A program may use at most 64 MiB of HBM per device.

v0:
```python
import jax
import jax.numpy as jnp
from jax import lax
from jax.sharding import PartitionSpec as P


def settle(values, source, dev_count):
    width = values.shape[0]
    block_len = values.shape[1] // dev_count
    blocks = values.reshape(width, dev_count, block_len)
    return jnp.take(blocks, source, axis=1).reshape(width, dev_count * block_len)


def local(u_fem, resid_fem, slot_map, restart, coeff):
    highest = lax.Precision.HIGHEST
    dev_count = lax.axis_size(("rows", "sub"))
    nrows_all = u_fem.shape[1] * dev_count
    source = jnp.argsort(slot_map[0])
    basis_rows, resid_row = (u_fem, resid_fem)
    gram_local = jnp.einsum("kn,jn->kj", basis_rows, basis_rows, precision=highest)
    inner_local = jnp.einsum("kn,n->k", basis_rows, resid_row[0], precision=highest)
    gram_sum = lax.psum(gram_local, ("rows", "sub"))
    chol_lower = jnp.linalg.cholesky(gram_sum / nrows_all)
    factor = lax.linalg.triangular_solve(
        chol_lower, restart, left_side=True, lower=True, transpose_a=True
    )
    new_rows = jnp.einsum("kp,kn->pn", factor, basis_rows, precision=highest)
    inner_prod = lax.psum(inner_local, ("rows", "sub"))
    half_solve = lax.linalg.triangular_solve(
        chol_lower, inner_prod[:, None], left_side=True, lower=True
    )
    proj_coef = (
        lax.linalg.triangular_solve(
            chol_lower, half_solve, left_side=True, lower=True, transpose_a=True
        )[:, 0]
        / nrows_all
    )
    remainder = resid_row - jnp.einsum("k,kn->n", proj_coef, basis_rows, precision=highest)[None, :]
    norm_sum = lax.psum(jnp.sum(remainder * remainder), ("rows", "sub"))
    next_row = remainder * lax.rsqrt(norm_sum / nrows_all + 1e-06)
    new_rows, next_row = (
        lax.all_to_all(new_rows, ("rows", "sub"), split_axis=1, concat_axis=1, tiled=True),
        lax.all_to_all(next_row, ("rows", "sub"), split_axis=1, concat_axis=1, tiled=True),
    )
    new_rows = settle(new_rows, source, dev_count)
    next_row = settle(next_row, source, dev_count)
    raised = jnp.dot(chol_lower, restart, precision=highest)
    coeff_all = lax.all_gather(coeff, "sub", axis=2, tiled=True)
    rotated = jnp.einsum("kp,ikm->ipm", raised, coeff_all, precision=highest)
    new_coeff = rotated * lax.rsqrt(jnp.mean(rotated * rotated) + 1e-06)
    return (new_rows, next_row, new_coeff)


def solution(mesh):
    in_specs = (
        P(None, ("rows", "sub")),
        P(None, ("rows", "sub")),
        P(("rows", "sub"), None),
        P(),
        P(None, None, "sub"),
    )
    out_specs = (P(None, ("rows", "sub")), P(None, ("rows", "sub")), P())
    return jax.shard_map(local, mesh=mesh, in_specs=in_specs, out_specs=out_specs, check_vma=False)
```

profile of v0, /device:TPU:0, one launch (start us, length us, event | category | flops | bytes accessed | tf_op | source)
XLA Modules:
  0.0 229.9 jit_solution(9403381852364649270)
XLA Ops:
  0.6 0.0 copy-start
  0.6 0.0 copy-start.1
  0.7 0.0 copy-start.2
  0.7 10.1 %fusion.16 = f32[120,120]{0,1:T(8,128)S(1)} fusion(f32[120,16384]{1,0:T(8,128)} %param.5), kind=kOutput, calls=%fused_computation.44 | convolution fusion | flops 2831155200 | bytes 7921920 | tf_op jit(solution)/shard_map/kn,jn->kj/dot_general | solution.py:20
  10.7 0.0 copy-done.1
  10.7 0.0 copy-done.2
  10.8 6.2 %convolution_bitcast_fusion.3 = f32[120]{0:T(128)S(1)} fusion(f32[120,16384]{1,0:T(8,128)S(1)} %copy-done.1, f32[1,16384]{1,0:T(1,128)S(1)} %copy-done.2), kind=kOutput, calls=%fused_computation.10 | convolution fusion | flops 23592960 | bytes 7930336 | tf_op jit(solution)/shard_map/kn,n->k/dot_general | solution.py:21
  16.9 42.8 %all-reduce = (f32[120,120]{0,1:T(8,128)S(1)}, f32[120]{0:T(128)S(1)}) all-reduce(f32[120,120]{0,1:T(8,128)S(1)} %fusion.16, f32[120]{0:T(128)S(1)} %convolution_bitcast_fusion.3), channel_id=1, replica_groups=mesh['rows'=8,'sub'=4] {'rows','sub'}, use_global_device_ids=true, to_apply=%region_1.2 | all-reduce | flops 14520 | bytes 116160 | tf_op jit(solution)/shard_map/psum | solution.py:22
  59.8 0.1 copy.18
  59.9 11.0 %cholesky.16 = f32[120,120]{1,0:T(8,128)S(1)} custom-call(f32[120,120]{1,0:T(8,128)S(1)} %fusion.9), custom_call_target="Cholesky" | custom-call | tf_op jit(solution)/shard_map/jit(cholesky)/cholesky | solution.py:23
  70.9 0.6 compare_reduce_fusion
  71.5 0.7 select_bitcast_fusion
  72.2 9.2 %custom-call.10 = f32[1,120,120]{1,2,0:T(8,128)S(1)} custom-call(f32[1,120,120]{2,1,0:T(8,128)S(1)} %select_bitcast_fusion), custom_call_target="InvertDiagBlocksLowerTriangular" | custom-call | tf_op jit(solution)/shard_map/triangular_solve | solution.py:24
  81.4 0.2 convolution_bitcast_fusion.2
  81.6 0.2 fusion.1
  81.8 6.7 %multiply_reduce_fusion = (f32[]{:T(128)}, f32[1,16384]{1,0:T(1,128)S(1)}) fusion(f32[1,16384]{1,0:T(1,128)S(1)} %copy-done.2, f32[120,1]{0,1:T(1,128)S(1)} %fusion.1, f32[120,16384]{1,0:T(8,128)} %param.5), kind=kOutput, calls=%fused_computation.15 | convolution fusion | flops 23642112 | bytes 7995876 | tf_op jit(solution)/shard_map/k,kn->n/dot_general | solution.py:38
  88.5 40.3 %psum.23 = f32[]{:T(128)} all-reduce(f32[]{:T(128)} %get-tuple-element.7), channel_id=1, replica_groups=mesh['rows'=8,'sub'=4] {'rows','sub'}, use_global_device_ids=true, to_apply=%region_6.7 | all-reduce | flops 1 | bytes 8 | tf_op jit(solution)/shard_map/psum | solution.py:39
  129.5 0.7 broadcast_multiply_fusion
  130.1 5.4 %all-to-all-start.1 = ((f32[1,32,512]{2,0,1:T(1,128)}), f32[1,32,512]{2,0,1:T(1,128)S(1)}, u32[]{:S(2)}, u32[]{:S(2)}) async-start(f32[1,32,512]{2,0,1:T(1,128)} %bitcast.14), calls=%async_computation.1 | async-start | bytes 131072 | tf_op jit(solution)/shard_map/all_to_all | solution.py:43
  135.5 0.0 copy-done
  135.6 0.2 fusion.7
  135.8 0.0 copy-start.4
  135.8 6.5 %fusion.17 = f32[40,16384]{1,0:T(8,128)S(1)} fusion(f32[120,40]{0,1:T(8,128)S(1)} %fusion.7, f32[120,16384]{1,0:T(8,128)} %param.5), kind=kOutput, calls=%fused_computation.45 | convolution fusion | flops 943718400 | bytes 10504960 | tf_op jit(solution)/shard_map/kp,kn->pn/dot_general | solution.py:27
  142.3 0.0 copy-start.3
  142.3 1.7 copy.36
  144.1 0.0 copy-done.4
  144.1 1.7 sort.17
  145.8 0.0 all-to-all-done.1
  145.8 5.8 %all-to-all-start = ((f32[40,32,512]{2,0,1:T(8,128)}), f32[40,32,512]{2,0,1:T(8,128)S(1)}, u32[]{:S(2)}, u32[]{:S(2)}) async-start(f32[40,32,512]{2,0,1:T(8,128)} %bitcast.69), calls=%async_computation | async-start | bytes 5242880 | tf_op jit(solution)/shard_map/all_to_all | solution.py:42
  151.6 0.1 broadcast_bitcast_fusion
  151.7 0.1 copy.28
  151.8 0.0 copy-done.3
  151.8 67.3 %all_gather.3 = f32[3,120,120]{1,0,2:T(4,128)S(1)} all-gather(f32[3,120,30]{1,0,2:T(4,128)S(1)} %copy.21), channel_id=1, replica_groups=mesh['rows'=8,'sub'=4] {'sub'}, dimensions={2}, use_global_device_ids=true | all-gather | bytes 216000 | tf_op jit(solution)/shard_map/all_gather | solution.py:48
  219.1 0.9 convolution_bitcast_fusion
  220.0 1.0 multiply_reduce_fusion.1
  221.8 0.1 broadcast_bitcast_fusion.1
  221.9 0.6 multiply_bitcast_fusion
  222.5 0.6 gather_fusion.1
  223.1 0.1 copy.29
  223.2 0.7 broadcast_select_fusion.1
  223.9 0.0 all-to-all-done
  223.9 2.2 gather_fusion
  226.2 2.1 copy.26
  228.2 1.7 broadcast_select_fusion
  (10 shorter events, 0.1 us)
Async XLA Ops:
  0.6 134.9 %copy-start = (f32[120,40]{0,1:T(8,128)S(1)}, f32[120,40]{0,1:T(8,128)}, u32[]{:S(2)}) copy-start(f32[120,40]{0,1:T(8,128)} %param.8) | copy-start | bytes 57604
  0.6 10.1 %copy-start.1 = (f32[120,16384]{1,0:T(8,128)S(1)}, f32[120,16384]{1,0:T(8,128)}, u32[]{:S(2)}) copy-start(f32[120,16384]{1,0:T(8,128)} %param.5) | copy-start | bytes 23592964
  0.7 10.1 %copy-start.2 = (f32[1,16384]{1,0:T(1,128)S(1)}, f32[1,16384]{1,0:T(1,128)}, u32[]{:S(2)}) copy-start(f32[1,16384]{1,0:T(1,128)} %param.6) | copy-start | bytes 196612
  130.1 15.6 %all-to-all-start.1 = ((f32[1,32,512]{2,0,1:T(1,128)}), f32[1,32,512]{2,0,1:T(1,128)S(1)}, u32[]{:S(2)}, u32[]{:S(2)}) async-start(f32[1,32,512]{2,0,1:T(1,128)} %bitcast.14), calls=%async_computation.1 | async-start | bytes 131072 | tf_op jit(solution)/shard_map/all_to_all | solution.py:43
  135.8 8.3 %copy-start.4 = (s32[1,32]{1,0:T(1,128)S(1)}, s32[1,32]{1,0:T(1,128)}, u32[]{:S(2)}) copy-start(s32[1,32]{1,0:T(1,128)} %param.7) | copy-start | bytes 388
  142.3 9.4 %copy-start.3 = (f32[3,120,30]{1,2,0:T(8,128)S(1)}, f32[3,120,30]{1,2,0:T(8,128)}, u32[]{:S(2)}) copy-start(f32[3,120,30]{1,2,0:T(8,128)} %param.9) | copy-start | bytes 129604
  145.8 78.2 %all-to-all-start = ((f32[40,32,512]{2,0,1:T(8,128)}), f32[40,32,512]{2,0,1:T(8,128)S(1)}, u32[]{:S(2)}, u32[]{:S(2)}) async-start(f32[40,32,512]{2,0,1:T(8,128)} %bitcast.69), calls=%async_computation | async-start | bytes 5242880 | tf_op jit(solution)/shard_map/all_to_all | solution.py:42
where the time goes:
time: 231 us; the launch traced here: 230 us
  blocking collectives  150 us (65%)
  matrix products  32 us (14%)
  other arithmetic  27 us (12%)
  starting transfers between devices  11.2 us (5%)
  local copies, waits for them, and re-layouts  7.06 us (3%)
    all_gather x1, blocking collectives, local(): coeff_all = lax.all_gather(coeff, 'sub', axis=2, tiled=True)  67.3 us
    psum x1, blocking collectives, local(): gram_sum = lax.psum(gram_local, ('rows', 'sub'))  42.8 us
    psum x1, blocking collectives, local(): norm_sum = lax.psum(jnp.sum(remainder * remainder), ('rows', 'sub'))  40.3 us
    another operation x3, other arithmetic, local(): chol_lower = jnp.linalg.cholesky(gram_sum / nrows_all)  11.6 us
    dot_general x1, matrix products, local(): jnp.einsum('kn,jn->kj', basis_rows, basis_rows, precision=highest)  10.1 us
    another operation x2, other arithmetic, local(): lax.linalg.triangular_solve(chol_lower, restart, left_side=True, lower=Tr...  9.85 us
    dot_general x1, matrix products, local(): jnp.einsum('k,kn->n', proj_coef, basis_rows, precision=highest)[None, :]  6.74 us
    dot_general x1, matrix products, local(): new_rows = jnp.einsum('kp,kn->pn', factor, basis_rows, precision=highest)  6.51 us
  transfers between devices with their start and end apart: 2, of which 0 were waited for; matrix products, arithmetic and copies ran while one was open for 6% of the time, Pallas kernels for 0%

commit v1 on v0

--- a/solution.py
+++ b/solution.py
@@ -19,7 +19,8 @@
     basis_rows, resid_row = (u_fem, resid_fem)
     gram_local = jnp.einsum("kn,jn->kj", basis_rows, basis_rows, precision=highest)
     inner_local = jnp.einsum("kn,n->k", basis_rows, resid_row[0], precision=highest)
-    gram_sum = lax.psum(gram_local, ("rows", "sub"))
+    partial = lax.psum(gram_local, "sub")
+    gram_sum = lax.psum(partial, "rows")
     chol_lower = jnp.linalg.cholesky(gram_sum / nrows_all)
     factor = lax.linalg.triangular_solve(
         chol_lower, restart, left_side=True, lower=True, transpose_a=True

time: 231 us -> 272 us (1.18)
  blocking collectives: 150 us -> 191 us
    psum x1 -> x3, blocking collectives: 42.8 us -> 82 us  [the longest x1 37.5 us: local(): inner_prod = lax.psum(inner_local, ('rows', 'sub'))]
  transfers between devices with their start and end apart: 2 -> 2, of which waited for: 0 -> 0; matrix products, arithmetic and copies ran while one was open for 6% -> 5% of each run, Pallas kernels for 0% -> 0%
where the time goes in v1:
time: 272 us; the launch traced here: 271 us
  blocking collectives  191 us (70%)
  matrix products  34.1 us (13%)
  other arithmetic  27 us (10%)
  starting transfers between devices  9.65 us (4%)
  local copies, waits for them, and re-layouts  6.97 us (3%)
    all_gather x1, blocking collectives, local(): coeff_all = lax.all_gather(coeff, 'sub', axis=2, tiled=True)  67.3 us
    psum x1, blocking collectives, local(): norm_sum = lax.psum(jnp.sum(remainder * remainder), ('rows', 'sub'))  41.8 us
    psum x1, blocking collectives, local(): inner_prod = lax.psum(inner_local, ('rows', 'sub'))  37.5 us
    psum x1, blocking collectives, local(): gram_sum = lax.psum(partial, 'rows')  22.9 us
    psum x1, blocking collectives, local(): partial = lax.psum(gram_local, 'sub')  21.6 us
    another operation x3, other arithmetic, local(): chol_lower = jnp.linalg.cholesky(gram_sum / nrows_all)  11.6 us
    dot_general x1, matrix products, local(): jnp.einsum('kn,jn->kj', basis_rows, basis_rows, precision=highest)  9.95 us
    another operation x2, other arithmetic, local(): lax.linalg.triangular_solve(chol_lower, restart, left_side=True, lower=Tr...  9.85 us
  transfers between devices with their start and end apart: 2, of which 0 were waited for; matrix products, arithmetic and copies ran while one was open for 5% of the time, Pallas kernels for 0%

profile of v1, /device:TPU:0, one launch (start us, length us, event | category | flops | bytes accessed | tf_op | source)
XLA Modules:
  0.0 271.1 jit_solution(6865496560005572942)
XLA Ops:
  0.6 0.0 copy-start
  0.6 0.0 copy-start.1
  0.7 9.9 %fusion.16 = f32[120,120]{0,1:T(8,128)S(1)} fusion(f32[120,16384]{1,0:T(8,128)} %param.5), kind=kOutput, calls=%fused_computation.44 | convolution fusion | flops 2831155200 | bytes 7921920 | tf_op jit(solution)/shard_map/kn,jn->kj/dot_general | solution.py:20
  10.6 21.6 %psum.28 = f32[120,120]{0,1:T(8,128)S(1)} all-reduce(f32[120,120]{0,1:T(8,128)S(1)} %fusion.16), channel_id=1, replica_groups=mesh['rows'=8,'sub'=4] {'sub'}, use_global_device_ids=true, to_apply=%region_1.2 | all-reduce | flops 14400 | bytes 115200 | tf_op jit(solution)/shard_map/psum | solution.py:22
  32.2 22.9 %psum.29 = f32[120,120]{0,1:T(8,128)S(1)} all-reduce(f32[120,120]{0,1:T(8,128)S(1)} %psum.28), channel_id=1, replica_groups=mesh['rows'=8,'sub'=4] {'rows'}, use_global_device_ids=true, to_apply=%region_2.3 | all-reduce | flops 14400 | bytes 115200 | tf_op jit(solution)/shard_map/psum | solution.py:23
  55.2 0.1 copy.18
  55.3 11.0 %cholesky.16 = f32[120,120]{1,0:T(8,128)S(1)} custom-call(f32[120,120]{1,0:T(8,128)S(1)} %fusion.9), custom_call_target="Cholesky" | custom-call | tf_op jit(solution)/shard_map/jit(cholesky)/cholesky | solution.py:24
  66.3 0.6 compare_reduce_fusion
  66.9 0.7 select_bitcast_fusion
  67.6 9.2 %custom-call.10 = f32[1,120,120]{1,2,0:T(8,128)S(1)} custom-call(f32[1,120,120]{2,1,0:T(8,128)S(1)} %select_bitcast_fusion), custom_call_target="InvertDiagBlocksLowerTriangular" | custom-call | tf_op jit(solution)/shard_map/triangular_solve | solution.py:25
  76.8 0.0 copy-done.1
  76.8 8.4 %convolution_bitcast_fusion.3 = f32[120]{0:T(128)S(1)} fusion(f32[120,16384]{1,0:T(8,128)} %param.5, f32[1,16384]{1,0:T(1,128)S(1)} %copy-done.1), kind=kOutput, calls=%fused_computation.10 | convolution fusion | flops 23592960 | bytes 7930336 | tf_op jit(solution)/shard_map/kn,n->k/dot_general | solution.py:21
  85.2 37.5 %psum.30 = f32[120]{0:T(128)S(1)} all-reduce(f32[120]{0:T(128)S(1)} %convolution_bitcast_fusion.3), channel_id=1, replica_groups=mesh['rows'=8,'sub'=4] {'rows','sub'}, use_global_device_ids=true, to_apply=%region_5.6 | all-reduce | flops 120 | bytes 960 | tf_op jit(solution)/shard_map/psum | solution.py:29
  122.7 0.2 convolution_bitcast_fusion.2
  122.9 0.2 fusion.1
  123.1 6.7 %multiply_reduce_fusion = (f32[]{:T(128)}, f32[1,16384]{1,0:T(1,128)S(1)}) fusion(f32[1,16384]{1,0:T(1,128)S(1)} %copy-done.1, f32[120,1]{0,1:T(1,128)S(1)} %fusion.1, f32[120,16384]{1,0:T(8,128)} %param.5), kind=kOutput, calls=%fused_computation.15 | convolution fusion | flops 23642112 | bytes 7995876 | tf_op jit(solution)/shard_map/k,kn->n/dot_general | solution.py:39
  129.8 41.8 %psum.31 = f32[]{:T(128)} all-reduce(f32[]{:T(128)} %get-tuple-element.5), channel_id=1, replica_groups=mesh['rows'=8,'sub'=4] {'rows','sub'}, use_global_device_ids=true, to_apply=%region_7.8 | all-reduce | flops 1 | bytes 8 | tf_op jit(solution)/shard_map/psum | solution.py:40
  172.4 0.7 broadcast_multiply_fusion
  173.0 3.8 %all-to-all-start.1 = ((f32[1,32,512]{2,0,1:T(1,128)}), f32[1,32,512]{2,0,1:T(1,128)S(1)}, u32[]{:S(2)}, u32[]{:S(2)}) async-start(f32[1,32,512]{2,0,1:T(1,128)} %bitcast.14), calls=%async_computation.1 | async-start | bytes 131072 | tf_op jit(solution)/shard_map/all_to_all | solution.py:44
  176.9 0.0 copy-done
  176.9 0.2 fusion.7
  177.1 0.0 copy-start.3
  177.1 6.5 %fusion.17 = f32[40,16384]{1,0:T(8,128)S(1)} fusion(f32[120,40]{0,1:T(8,128)S(1)} %fusion.7, f32[120,16384]{1,0:T(8,128)} %param.5), kind=kOutput, calls=%fused_computation.45 | convolution fusion | flops 943718400 | bytes 10504960 | tf_op jit(solution)/shard_map/kp,kn->pn/dot_general | solution.py:28
  183.6 0.0 copy-start.2
  183.7 1.7 copy.36
  185.4 0.0 copy-done.3
  185.4 1.7 sort.17
  187.1 0.0 all-to-all-done.1
  187.1 5.8 %all-to-all-start = ((f32[40,32,512]{2,0,1:T(8,128)}), f32[40,32,512]{2,0,1:T(8,128)S(1)}, u32[]{:S(2)}, u32[]{:S(2)}) async-start(f32[40,32,512]{2,0,1:T(8,128)} %bitcast.69), calls=%async_computation | async-start | bytes 5242880 | tf_op jit(solution)/shard_map/all_to_all | solution.py:43
  192.9 0.1 broadcast_bitcast_fusion
  193.0 0.1 copy.28
  193.1 0.0 copy-done.2
  193.1 67.3 %all_gather.3 = f32[3,120,120]{1,0,2:T(4,128)S(1)} all-gather(f32[3,120,30]{1,0,2:T(4,128)S(1)} %copy.21), channel_id=1, replica_groups=mesh['rows'=8,'sub'=4] {'sub'}, dimensions={2}, use_global_device_ids=true | all-gather | bytes 216000 | tf_op jit(solution)/shard_map/all_gather | solution.py:49
  260.4 0.9 convolution_bitcast_fusion
  261.3 1.0 multiply_reduce_fusion.1
  263.1 0.1 broadcast_bitcast_fusion.1
  263.2 0.6 multiply_bitcast_fusion
  263.8 0.6 gather_fusion.1
  264.4 0.1 copy.29
  264.5 0.7 broadcast_select_fusion.1
  265.3 0.0 all-to-all-done
  265.3 2.2 gather_fusion
  267.5 2.0 copy.26
  269.4 1.7 broadcast_select_fusion
  (10 shorter events, 0.1 us)
Async XLA Ops:
  0.6 176.2 %copy-start = (f32[120,40]{0,1:T(8,128)S(1)}, f32[120,40]{0,1:T(8,128)}, u32[]{:S(2)}) copy-start(f32[120,40]{0,1:T(8,128)} %param.8) | copy-start | bytes 57604
  0.6 76.2 %copy-start.1 = (f32[1,16384]{1,0:T(1,128)S(1)}, f32[1,16384]{1,0:T(1,128)}, u32[]{:S(2)}) copy-start(f32[1,16384]{1,0:T(1,128)} %param.6) | copy-start | bytes 196612
  173.0 14.1 %all-to-all-start.1 = ((f32[1,32,512]{2,0,1:T(1,128)}), f32[1,32,512]{2,0,1:T(1,128)S(1)}, u32[]{:S(2)}, u32[]{:S(2)}) async-start(f32[1,32,512]{2,0,1:T(1,128)} %bitcast.14), calls=%async_computation.1 | async-start | bytes 131072 | tf_op jit(solution)/shard_map/all_to_all | solution.py:44
  177.1 8.3 %copy-start.3 = (s32[1,32]{1,0:T(1,128)S(1)}, s32[1,32]{1,0:T(1,128)}, u32[]{:S(2)}) copy-start(s32[1,32]{1,0:T(1,128)} %param.7) | copy-start | bytes 388
  183.6 9.4 %copy-start.2 = (f32[3,120,30]{1,2,0:T(8,128)S(1)}, f32[3,120,30]{1,2,0:T(8,128)}, u32[]{:S(2)}) copy-start(f32[3,120,30]{1,2,0:T(8,128)} %param.9) | copy-start | bytes 129604
  187.1 78.2 %all-to-all-start = ((f32[40,32,512]{2,0,1:T(8,128)}), f32[40,32,512]{2,0,1:T(8,128)S(1)}, u32[]{:S(2)}, u32[]{:S(2)}) async-start(f32[40,32,512]{2,0,1:T(8,128)} %bitcast.69), calls=%async_computation | async-start | bytes 5242880 | tf_op jit(solution)/shard_map/all_to_all | solution.py:43
